TPU v7x, 512 devices: a 8x2x16 block of a 8x8x16 slice. The times are simulated.
512 devices in a mesh: grp: 2 (over y), tp: 128 (over x, z), sub: 2 (over core).
Axes of the slice: x: 8, y: 2, z: 16, core: 2. Of those that a mesh axis runs over, the one named last changes fastest.
The devices are a block of a 8x8x16 slice.
Arguments:
- hidden_in: bfloat16 [32, 2, 4096], P('grp', 'sub', 'tp'), parts along dimension 0, may hold values from -16 to 16
- norm_attn: float32 [8192], replicated, may hold values from 0.25 to 1.75
- w_query: bfloat16 [8192, 2, 4096], P(None, 'sub', 'tp'), may hold values from -0.0625 to 0.0625
- w_key: bfloat16 [8192, 2, 512], P(None, 'sub', 'tp'), may hold values from -0.0625 to 0.0625
- w_value: bfloat16 [8192, 2, 512], P(None, 'sub', 'tp'), may hold values from -0.0625 to 0.0625
- w_out: bfloat16 [2, 4096, 2, 4096], P('sub', None, None, 'tp'), may hold values from -0.0625 to 0.0625
- norm_ffn: float32 [8192], replicated, may hold values from 0.25 to 1.75
- w_gate: bfloat16 [2, 4096, 14336], P('sub', None, 'tp'), may hold values from -0.0625 to 0.0625
- w_up: bfloat16 [2, 4096, 14336], P('sub', None, 'tp'), may hold values from -0.0625 to 0.0625
- w_down: bfloat16 [14336, 2, 4096], P('tp', 'sub'), may hold values from -0.1875 to 0.1875
- cache_keys: bfloat16 [32, 1024, 8, 128], P('grp', 'tp', 'sub'), parts along dimension 0, may hold values from -250 to 250
- cache_values: bfloat16 [32, 1024, 8, 128], P('grp', 'tp', 'sub'), parts along dimension 0, may hold values from -6 to 6
- lengths: int32 [32], P('grp'), parts along dimension 0, may hold values from 1 to 1024, as said below
Outputs:
- hidden_out: bfloat16 [32, 2, 4096], P('grp', 'sub', 'tp'), parts along dimension 0
There are 2 independent parts, one for each index of `grp`. A program takes and returns all parts, laid end to end along the dimension named above; an argument that names none is the same for every part. Nothing has to cross between parts.
Inputs may be any that keep to these rules, and one draw needn't show every extreme that they name: `lengths`: some sequence has 1024 live positions and some has 1.
All inputs are finite; a program needn't handle non-finite values.
Results may differ from a plain program's by a relative error of at most 0.012.
The roundings to bfloat16 on the way count: a program that leaves them out, or rounds other values in their place, can miss the bound.
Values may be sent and summed in bfloat16 or wider, within the bound.
A program may use at most 128 MiB of HBM per device.

v0:
```python
import math

import jax
import jax.numpy as jnp
from jax import lax
from jax.sharding import Mesh
from jax.sharding import PartitionSpec as P

HD = 128
TP = ("tp_0", "tp_1")


epsilon = 1e-05
rope_base = 500000.0
floor_score = -1e30


def joined_along(parts, dim):
    shape = list(parts.shape[1:])
    shape[dim] *= parts.shape[0]
    return jnp.moveaxis(parts, 0, dim).reshape(shape)


def gather_in_order(array, axes, sequence):
    parts = array[None]
    for k in sequence:
        parts = lax.all_gather(parts, axes[k], axis=0, tiled=True)
    carried = [lax.axis_size(axes[k]) for k in reversed(sequence)]
    parts = parts.reshape(*carried, *array.shape)
    turned = sorted(range(len(sequence)), key=lambda place: sequence[len(sequence) - 1 - place])
    return parts.transpose(*turned, *range(len(sequence), parts.ndim)).reshape(-1, *array.shape)


def whole_of(array, axes, sequence, dim):
    return joined_along(gather_in_order(array, axes, sequence), dim)


def sent_to_all(array, axis):
    copies = jnp.broadcast_to(array, (lax.axis_size(axis), *array.shape))
    return lax.all_to_all(copies, axis, split_axis=0, concat_axis=0, tiled=True)


def gathered_copies(array, axis, dim):
    parts = sent_to_all(array, axis)
    return joined_along(parts, dim)


def side_by_side(arrays, axis, dim, along):
    both = jnp.concatenate(arrays, axis=along)
    filled, at, gathered = (lax.all_gather(both, axis, axis=dim, tiled=True), 0, [])
    for a in arrays:
        gathered.append(lax.slice_in_dim(filled, at, at + a.shape[along], axis=along))
        at += a.shape[along]
    return tuple(gathered)


def collected_together(array, axis):
    leaves = jax.tree.leaves(array)
    sequence = sorted(range(len(leaves)), key=lambda k: -leaves[k].size)
    width = (1, *leaves[sequence[0]].shape)[-1]
    lines = [
        jnp.pad(leaves[k].reshape(-1), (0, -leaves[k].size % width)).reshape(-1, width)
        for k in sequence
    ]
    both, at, found = (lax.all_gather(jnp.concatenate(lines), axis), 0, {})
    for k, line in zip(sequence, lines):
        section = both[:, at : at + len(line)].reshape(len(both), -1)
        found[k] = section[:, : leaves[k].size].reshape(-1, *leaves[k].shape)
        at += len(line)
    numbers = iter(range(len(leaves)))
    return jax.tree.map(lambda _: found[next(numbers)], array)


def combined_by_axis(array, axes, combine):
    for axis in axes:
        pieces = collected_together(array, axis)
        array = jax.tree.map(lambda part: part[0], pieces)
        for k in range(1, lax.axis_size(axis)):
            array = combine(array, jax.tree.map(lambda part: part[k], pieces))
    return array


def cut_along(array, dim, size):
    shape = array.shape
    parts = array.reshape(*shape[:dim], size, shape[dim] // size, *shape[dim + 1 :])
    return jnp.moveaxis(parts, dim, 0)


def sum_at_owner(array, axis, dim):
    parts = cut_along(array, dim, lax.axis_size(axis))
    arrived = lax.all_to_all(parts, axis, split_axis=0, concat_axis=0, tiled=True)
    return arrived.sum(axis=0)


def over_pieces(array, axis):
    return lax.all_gather(array, axis).sum(0)


def over_copies(array, axis):
    return sent_to_all(array, axis).sum(axis=0)


def in_one(arrays, axis):
    vector, at, gathered = (jnp.concatenate([a.reshape(-1) for a in arrays]), 0, [])
    so_far = over_copies(vector, axis)
    for a in arrays:
        gathered.append(so_far[at : at + a.size].reshape(a.shape))
        at += a.size
    return tuple(gathered)


def summed_rows(array, axes, dim):
    for axis in axes:
        array = lax.psum_scatter(array, axis, scatter_dimension=dim, tiled=True)
    return array


def rope_angles(lengths):
    frequencies = rope_base ** (-(jnp.arange(HD // 2, dtype=jnp.float32) * 2.0) / HD)
    return lengths.astype(jnp.float32)[:, None] * frequencies[None, :]


def rotate(vectors, angles):
    middle_index = vectors.shape[-1] // 2
    cosine = jnp.cos(angles)[:, None, :]
    sine = jnp.sin(angles)[:, None, :]
    lower = vectors[..., :middle_index]
    upper = vectors[..., middle_index:]
    return jnp.concatenate([lower * cosine - upper * sine, upper * cosine + lower * sine], axis=-1)


def spread_rows(shard):
    across = whole_of(shard, TP, (0, 1), 2)
    return gathered_copies(across, "sub", 1)


def half_rows_of(shard):
    return whole_of(shard, TP, (0, 1), 2)


def join_partials(earlier, later):
    earlier_max, earlier_sum, earlier_out = earlier
    later_max, later_sum, later_out = later
    highest = jnp.maximum(earlier_max, later_max)
    earlier_scale = jnp.exp(earlier_max - highest)
    later_scale = jnp.exp(later_max - highest)
    joined_sum = earlier_sum * earlier_scale + later_sum * later_scale
    joined_out = earlier_out * earlier_scale[..., None] + later_out * later_scale[..., None]
    return (highest, joined_sum, joined_out)


def per_device(
    hidden_in,
    norm_attn,
    w_query,
    w_key,
    w_value,
    w_out,
    norm_ffn,
    w_gate,
    w_up,
    w_down,
    cache_keys,
    cache_values,
    lengths,
):
    seq_count = hidden_in.shape[0]
    shard_width = hidden_in.shape[2]
    half_width = shard_width * lax.axis_size(TP)
    model_width = half_width * lax.axis_size("sub")
    tp_pos = lax.axis_index(TP)
    sub_pos = lax.axis_index("sub")
    residual = hidden_in.astype(jnp.float32)
    whole_rows = spread_rows(hidden_in).astype(jnp.float32)
    factor = lax.rsqrt(jnp.mean(whole_rows * whole_rows, axis=(1, 2)) + epsilon)
    gain_whole = norm_attn.reshape(whole_rows.shape[1], half_width)
    gathered = (whole_rows * factor[:, None, None] * gain_whole).astype(jnp.bfloat16)
    flattened = gathered.reshape(seq_count, model_width)
    query_part = jnp.dot(
        flattened, w_query.reshape(model_width, -1), preferred_element_type=jnp.float32
    ).astype(jnp.bfloat16)
    key_part = jnp.dot(
        flattened, w_key.reshape(model_width, -1), preferred_element_type=jnp.float32
    ).astype(jnp.bfloat16)
    value_part = jnp.dot(
        flattened, w_value.reshape(model_width, -1), preferred_element_type=jnp.float32
    ).astype(jnp.bfloat16)
    query, key_new, value_new = (
        lax.all_gather(query_part, TP, axis=1, tiled=True),
        *side_by_side((key_part, value_part), TP, 1, 0),
    )
    query_heads = query.shape[1] // HD
    kv_heads = key_new.shape[1] // HD
    group_size = query_heads // kv_heads
    angles = rope_angles(lengths)
    query_rot = rotate(
        query.astype(jnp.float32).reshape(seq_count, query_heads, HD), angles
    ).astype(jnp.bfloat16)
    key_rot = rotate(key_new.astype(jnp.float32).reshape(seq_count, kv_heads, HD), angles).astype(
        jnp.bfloat16
    )
    grouped = query_rot.reshape(seq_count, kv_heads, group_size, HD)
    values_new = value_new.astype(jnp.float32).reshape(seq_count, kv_heads, 1, HD)
    span = cache_keys.shape[1]
    scores = jnp.einsum(
        "bkgd,blkd->bkgl", grouped, cache_keys, preferred_element_type=jnp.float32
    ) / math.sqrt(HD)
    places = tp_pos * span + jnp.arange(span, dtype=jnp.int32)
    live = (places[None, :] < lengths[:, None])[:, None, None, :]
    masked = jnp.where(live, scores, floor_score)
    local_max = jnp.max(masked, axis=-1)
    weights = jnp.where(live, jnp.exp(masked - local_max[..., None]), 0.0)
    local_sum = jnp.sum(weights, axis=-1)
    local_out = jnp.einsum(
        "bkgl,blkd->bkgd",
        weights,
        cache_values.astype(jnp.float32),
        precision=lax.Precision.HIGHEST,
    )
    own_score = jnp.sum(
        grouped.astype(jnp.float32) * key_rot.astype(jnp.float32)[:, :, None, :], axis=-1
    ) / math.sqrt(HD)
    joined_max, joined_sum, joined_out = combined_by_axis(
        (local_max, local_sum, local_out), TP, join_partials
    )
    highest = jnp.maximum(joined_max, own_score)
    kept_scale = jnp.exp(joined_max - highest)
    own_weight = jnp.exp(own_score - highest)
    numerator = joined_out * kept_scale[..., None] + own_weight[..., None] * values_new
    denominator = joined_sum * kept_scale + own_weight
    attended = (numerator / denominator[..., None]).reshape(seq_count, -1).astype(jnp.bfloat16)
    out_part = jnp.dot(
        attended, w_out.reshape(attended.shape[1], -1), preferred_element_type=jnp.float32
    )
    out_part = out_part.reshape(seq_count, -1, shard_width)
    mixed = sum_at_owner(out_part, "sub", 1)
    middle = (residual + mixed).astype(jnp.bfloat16)
    middle_float = middle.astype(jnp.float32)
    raw_half = half_rows_of(middle).astype(jnp.float32)
    partial_squares = jnp.sum(raw_half * raw_half, axis=(1, 2))
    squares_mid = over_pieces(partial_squares, "sub")
    factor_mid = lax.rsqrt(squares_mid / model_width + epsilon)
    gain_half = lax.dynamic_slice_in_dim(norm_ffn, sub_pos * half_width, half_width)
    half_rows = (raw_half * factor_mid[:, None, None] * gain_half).astype(jnp.bfloat16)
    half_flat = half_rows.reshape(seq_count, half_width)
    gate_part = jnp.dot(
        half_flat, w_gate.reshape(half_width, -1), preferred_element_type=jnp.float32
    )
    up_part = jnp.dot(half_flat, w_up.reshape(half_width, -1), preferred_element_type=jnp.float32)
    gate_total, up_total = in_one((gate_part, up_part), "sub")
    hidden = (jax.nn.silu(gate_total) * up_total).astype(jnp.bfloat16)
    down_part = jnp.dot(
        hidden, w_down.reshape(hidden.shape[1], -1), preferred_element_type=jnp.float32
    )
    down_share = summed_rows(down_part, TP, 1)
    return (middle_float + down_share[:, None, :]).astype(jnp.bfloat16)


def solution(mesh):
    split = Mesh(
        mesh.devices.reshape(mesh.shape["grp"], 8, 16, mesh.shape["sub"]),
        ("grp", "tp_0", "tp_1", "sub"),
    )
    return jax.shard_map(
        per_device,
        mesh=split,
        in_specs=(
            P("grp", "sub", TP),
            P(),
            P(None, "sub", TP),
            P(None, "sub", TP),
            P(None, "sub", TP),
            P("sub", None, None, TP),
            P(),
            P("sub", None, TP),
            P("sub", None, TP),
            P(TP, "sub", None),
            P("grp", TP, "sub", None),
            P("grp", TP, "sub", None),
            P("grp"),
        ),
        out_specs=P("grp", "sub", TP),
        check_vma=False,
    )
```

profile of v0, /device:TPU:80, one launch (start us, length us, event | category | flops | bytes accessed | tf_op | source)
XLA Modules:
  0.0 594.8 jit_solution(17651004225491951101)
XLA Ops:
  6.6 26.8 %all-gather = bf16[128,1,32]{2,0,1:T(8,128)(2,1)S(1)} all-gather(bf16[16,1,32]{2,0,1:T(8,128)(2,1)} %param.13), channel_id=2, replica_groups=mesh['grp'=2,'tp_0'=8,'tp_1'=16,'sub'=2] {'tp_0'}, dimensions={0}, use_global_device_ids=true | all-gather | bytes 9216 | tf_op jit(solution)/shard_map/all_gather | solution.py:27
  33.4 70.9 %all_gather.37 = bf16[128,16,1,32]{3,1,2,0:T(8,128)(2,1)S(1)} all-gather(bf16[8,16,1,32]{3,1,2,0:T(8,128)(2,1)S(1)} %bitcast.547), channel_id=1, replica_groups=mesh['grp'=2,'tp_0'=8,'tp_1'=16,'sub'=2] {'tp_1'}, dimensions={0}, use_global_device_ids=true | all-gather | bytes 139264 | tf_op jit(solution)/shard_map/all_gather | solution.py:27
  105.8 3.5 all-to-all-start
  111.8 87.3 %all-gather.5 = bf16[128,32,16]{1,2,0:T(8,128)(2,1)S(1)} all-gather(bf16[1,32,16]{1,2,0:T(8,128)(2,1)S(1)} %fusion.1), channel_id=1, replica_groups=mesh['grp'=2,'tp_0'=8,'tp_1'=16,'sub'=2] {'tp_0','tp_1'}, dimensions={0}, use_global_device_ids=true | all-gather | bytes 132096 | tf_op jit(solution)/shard_map/all_gather | solution.py:189
  202.9 37.7 %all-gather.10.cloned.1.call-done = f32[4160,128]{1,0:T(8,128)} async-done(((f32[520,128]{1,0:T(8,128)}), f32[4160,128]{1,0:T(8,128)}) %all-gather.10.cloned.1.call-update) | async-done | bytes 2129936 | tf_op jit(solution)/shard_map/all_gather | solution.py:65
  244.2 2.5 fusion.16
  248.2 90.2 %all-gather.6 = bf16[128,4,32]{2,1,0:T(4,128)(2,1)S(1)} all-gather(bf16[1,4,32]{2,1,0:T(4,128)(2,1)S(1)} %maximum_bitcast_fusion), channel_id=1, replica_groups=mesh['grp'=2,'tp_0'=8,'tp_1'=16,'sub'=2] {'tp_0','tp_1'}, dimensions={0}, use_global_device_ids=true | all-gather | bytes 33024 | tf_op jit(solution)/shard_map/all_gather | solution.py:50
  342.2 1.4 fusion.109
  343.6 1.5 fusion.108
  345.1 3.5 fusion.110
  348.6 1.4 squeeze.268
  350.0 1.4 squeeze.288
  351.3 1.4 squeeze.286
  354.1 1.4 squeeze.282
  355.5 1.4 squeeze.280
  356.8 1.4 squeeze.278
  358.2 1.4 squeeze.276
  359.6 1.4 squeeze.274
  361.0 1.4 squeeze.272
  362.4 1.4 squeeze.270
  366.4 1.4 squeeze.294
  367.8 1.4 squeeze.292
  369.2 1.4 squeeze.290
  372.0 1.4 squeeze.310
  373.3 1.4 squeeze.309
  374.7 1.4 squeeze.308
  376.1 1.4 squeeze.307
  377.5 1.4 squeeze.306
  378.9 1.4 squeeze.305
  381.6 1.4 squeeze.303
  383.0 1.4 squeeze.302
  384.4 1.4 squeeze.301
  385.8 1.4 squeeze.300
  387.2 1.4 squeeze.299
  388.6 1.4 squeeze.298
  389.9 1.4 squeeze.297
  393.9 1.7 multiply_add_fusion
  395.7 3.3 divide_convert_fusion
  399.9 1.5 fusion.113
  401.5 3.7 all_to_all.16
  407.2 24.7 %all-gather.3 = bf16[128,1,32]{2,0,1:T(8,128)(2,1)S(1)} all-gather(bf16[16,1,32]{2,0,1:T(8,128)(2,1)S(1)} %fusion.51), channel_id=5, replica_groups=mesh['grp'=2,'tp_0'=8,'tp_1'=16,'sub'=2] {'tp_0'}, dimensions={0}, use_global_device_ids=true | all-gather | bytes 9216 | tf_op jit(solution)/shard_map/all_gather | solution.py:27
  431.8 30.6 %all_gather.45 = bf16[128,16,1,32]{3,1,2,0:T(8,128)(2,1)S(1)} all-gather(bf16[8,16,1,32]{3,1,2,0:T(8,128)(2,1)S(1)} %bitcast.548), channel_id=1, replica_groups=mesh['grp'=2,'tp_0'=8,'tp_1'=16,'sub'=2] {'tp_1'}, dimensions={0}, use_global_device_ids=true | all-gather | bytes 139264 | tf_op jit(solution)/shard_map/all_gather | solution.py:27
  463.1 2.5 all-reduce
  467.4 1.6 fusion.7
  469.2 3.8 all_to_all.17
  474.2 38.7 %reduce-scatter.5.cloned.1.call-done = f32[16,512]{1,0:T(8,128)} async-done(((f32[16,4096]{1,0:T(8,128)}), f32[16,512]{1,0:T(8,128)}) %reduce-scatter.5.cloned.1.call-update) | async-done | bytes 32784 | tf_op jit(solution)/shard_map/reduce_scatter | solution.py:114
  512.9 1.6 copy.106
  514.5 72.4 %reduce-scatter.7.cloned.1.call-done = f32[32,16]{1,0:T(8,128)} async-done(((f32[512,16]{1,0:T(8,128)}), f32[32,16]{1,0:T(8,128)}) %reduce-scatter.7.cloned.1.call-update) | async-done | bytes 2064
  (125 shorter events, 33.4 us)
Async XLA Ops:
  6.5 466.6 %copy-start = (bf16[112,1,4096]{2,0,1:T(8,128)(2,1)S(1)}, bf16[112,1,4096]{2,0,1:T(8,128)(2,1)}, u32[]{:S(2)}) copy-start(bf16[112,1,4096]{2,0,1:T(8,128)(2,1)} %param.22) | copy-start | bytes 2752516
  33.4 76.0 %copy-start.14 = (s32[16]{0:T(128)S(1)}, s32[16]{0:T(128)}, u32[]{:S(2)}) copy-start(s32[16]{0:T(128)} %param.25) | copy-start | bytes 196
  33.4 76.1 %copy-start.12 = (f32[8192]{0:T(1024)S(1)}, f32[8192]{0:T(1024)}, u32[]{:S(2)}) copy-start(f32[8192]{0:T(1024)} %param.14) | copy-start | bytes 98308
  104.3 7.2 %copy-start.8 = (bf16[8192,1,32]{0,2,1:T(8,128)(2,1)S(1)}, bf16[8192,1,32]{0,2,1:T(8,128)(2,1)}, u32[]{:S(2)}) copy-start(bf16[8192,1,32]{0,2,1:T(8,128)(2,1)} %param.15) | copy-start | bytes 1572868
  105.8 5.0 all-to-all-start
  109.2 131.4 %all-gather.10.cloned.1.call-start = ((), (), s32[]{:S(2)}) async-start(), calls=%async_computation.6 | async-start | bytes 2396160 | tf_op jit(solution)/shard_map/all_gather | solution.py:65
  199.1 1.6 copy-start.10
  199.9 1.5 copy-start.11
  201.9 45.8 %copy-start.15 = (bf16[8192,1,4]{0,2,1:T(4,128)(2,1)S(1)}, bf16[8192,1,4]{0,2,1:T(4,128)(2,1)}, u32[]{:S(2)}) copy-start(bf16[8192,1,4]{0,2,1:T(4,128)(2,1)} %param.17) | copy-start | bytes 196612
  202.0 45.9 %copy-start.16 = (bf16[8192,1,4]{0,2,1:T(4,128)(2,1)S(1)}, bf16[8192,1,4]{0,2,1:T(4,128)(2,1)}, u32[]{:S(2)}) copy-start(bf16[8192,1,4]{0,2,1:T(4,128)(2,1)} %param.16) | copy-start | bytes 196612
  202.8 139.4 %all-gather.12.cloned.1.call-start = ((), (), s32[]{:S(2)}) async-start(), calls=%async_computation.7 | async-start | bytes 4526080 | tf_op jit(solution)/shard_map/all_gather | solution.py:65
  244.2 96.9 %copy-start.13 = (f32[8192]{0:T(1024)S(1)}, f32[8192]{0:T(1024)}, u32[]{:S(2)}) copy-start(f32[8192]{0:T(1024)} %param.19) | copy-start | bytes 98308
  247.5 265.4 %reduce-scatter.5.cloned.1.call-start = ((), (), s32[]{:S(2)}) async-start(), calls=%async_computation.5 | async-start | bytes 294912 | tf_op jit(solution)/shard_map/reduce_scatter | solution.py:114
  392.7 2.9 copy-start.1
  392.7 2.9 copy-start.2
  392.7 2.9 copy-start.3
  392.7 3.0 copy-start.4
  392.7 3.0 copy-start.5
  392.7 3.0 copy-start.6
  392.7 3.0 copy-start.9
  465.8 1.2 copy-start.7
  474.1 112.8 %reduce-scatter.7.cloned.1.call-start = ((), (), s32[]{:S(2)}) async-start(), calls=%async_computation.8 | async-start | bytes 278528
Sparse Core Ops, SparseCore 0:
  202.9 37.6 all-gather.9
  247.6 79.2 all-gather.11
  474.3 38.5 reduce-scatter.4
  515.5 71.3 reduce-scatter.6
where the time goes:
time: 598 us; the launch traced here: 595 us
  blocking collectives  341 us (57%)
  waiting for transfers between devices  150 us (25%)
  local copies, waits for them, and re-layouts  61.8 us (10%)
  other arithmetic  18.1 us (3%)
  between operations  14.3 us (2%)
    all_gather x4, blocking collectives, gather_in_order(): parts = lax.all_gather(parts, axes[k], axis=0, tiled=True)  153 us
    all_gather x1, blocking collectives, side_by_side(): lax.all_gather(both, axis, axis=dim, tiled=True)  90.2 us
    all_gather x1, blocking collectives, per_device(): lax.all_gather(query_part, TP, axis=1, tiled=True)  87.3 us
    unnamed x5, waiting for transfers between devices  72.6 us
    squeeze x30, local copies, waits for them, and re-layouts, combined_by_axis(): array = combine(array, jax.tree.map(lambda part: part[k], pieces))  41.3 us
    reduce_scatter x1, waiting for transfers between devices, summed_rows(): array = lax.psum_scatter(array, axis, scatter_dimension=dim, tiled=True)  38.7 us
    all_gather x2, waiting for transfers between devices, collected_together(): both, at, found = (lax.all_gather(jnp.concatenate(lines), axis), 0, {})  37.7 us
  transfers between devices with their start and end apart: 5, of which 4 were waited for; matrix products, arithmetic and copies ran while one was open for 1% of the time, Pallas kernels for 0%

commit v1 on v0

v1 whole, which is shorter than its diff:
```python
import math

import jax
import jax.numpy as jnp
import numpy as np
from jax import lax
from jax.experimental import pallas as pl
from jax.experimental.pallas import tpu as pltpu
from jax.sharding import PartitionSpec as P

HD = 128
NX, NZ = 8, 16
MESH = pl.DeviceIdType.MESH
EPS = 1e-05
ROPE_BASE = 500000.0
FLOOR = -1e30
F32, BF16 = jnp.float32, jnp.bfloat16

Z_ORDER = [8, 7, 9, 6, 10, 5, 11, 4, 12, 3, 13, 2, 14, 1, 15]
X_ORDER = [4, 3, 5, 2, 6, 1, 7]
X_ARRIVAL = [1, 7, 2, 6, 3, 5, 4]


def nt_dot(a, b):
    return lax.dot_general(a, b, (((1,), (1,)), ((), ())), preferred_element_type=F32)


def iota(shape, dim):
    return lax.broadcasted_iota(jnp.int32, shape, dim)


def block_transpose(t):
    turn = (iota(t.shape, 0) // 4 - iota(t.shape, 1) // 32 + 4) % 4
    out = t
    for d in range(1, 4):
        moved = pltpu.roll(pltpu.roll(t, 128 - 32 * d, axis=1), 4 * d, axis=0)
        out = jnp.where(turn == d, moved, out)
    return out


def widened(v, lanes=128):
    return jnp.concatenate([v, jnp.zeros((v.shape[0], lanes - v.shape[1]), v.dtype)], axis=1)


def cos_sin(angle):
    turns = jnp.floor(angle * (2.0 / math.pi) + 0.5)
    r = angle - turns * 1.5703125
    r = r - turns * 4.837512969970703125e-4
    r = r - turns * 7.54978995489188216e-8
    r2 = r * r
    sine = r + r * r2 * (-1.6666654611e-1 + r2 * (8.3321608736e-3 + r2 * -1.9515295891e-4))
    cosine = 1.0 - 0.5 * r2 + r2 * r2 * (
        4.166664568298827e-2 + r2 * (-1.388731625493765e-3 + r2 * 2.443315711809948e-5)
    )
    quarter = turns.astype(jnp.int32) & 3
    odd = (quarter & 1) == 1
    c = jnp.where(odd, sine, cosine)
    s = jnp.where(odd, cosine, sine)
    c = jnp.where((quarter == 1) | (quarter == 2), -c, c)
    s = jnp.where(quarter >= 2, -s, s)
    return c, s


def kernel(
    hid, gain_a, wq, wk, wv, wo, gain_f, wg, wu, wd, ck, cv, lens, freq,
    out,
    hid_v, ga_v, gf_v, wcat, wk_v, wv_v, wo_v, wg_v, wu_v, wd_v, kb, vb, kx, vx, len_v, freq_v,
    h1s, h1r, xall, qs, qr, qxs, qxr, ps, pr, ats, atr, axs, axr, mos, mor,
    mzs, mzr, mxs, mxr, ges, ger, dxs, dxr, dzs, dzr,
    local, ssem, rsem, xr_hid, xr_att, xr_mid, fwd_r,
):
    g, tp, s = lax.axis_index("grp"), lax.axis_index("tp"), lax.axis_index("sub")
    x, z = tp // NZ, tp % NZ
    seqs = hid_v.shape[0]
    half = wo_v.shape[1]
    block = half // NX

    def z_peer(o):
        return (z + o) % NZ

    def x_peer(o):
        return (x + o) % NX

    def at(px, pz):
        return (g, px * NZ + pz, s)

    partner = (g, tp, 1 - s)

    barrier = pltpu.get_barrier_semaphore()
    for o in Z_ORDER:
        pl.semaphore_signal(barrier, 1, device_id=at(x, z_peer(o)), device_id_type=MESH)
    for o in X_ORDER:
        pl.semaphore_signal(barrier, 1, device_id=at(x_peer(o), z), device_id_type=MESH)
    pl.semaphore_signal(barrier, 1, device_id=partner, device_id_type=MESH)

    def fetch(k, src, dst):
        copy = pltpu.make_async_copy(src, dst, local.at[k])
        copy.start()
        return copy

    got_hid = fetch(0, hid, hid_v)
    rows_q = wq.shape[0]
    span = ck.shape[1]
    got_first = [
        fetch(1, lens, len_v),
        fetch(2, freq, freq_v),
        fetch(3, wk, wk_v),
        fetch(4, wv, wv_v),
        fetch(5, wq, wcat.at[pl.ds(0, rows_q)]),
        fetch(6, gain_a, ga_v),
    ]
    got_cache = [
        fetch(7, ck.at[z], kb.at[z]),
        fetch(8, cv.at[z], vb.at[z]),
    ]
    got_later = [
        fetch(9, wo, wo_v),
        fetch(10, gain_f.at[:, pl.ds(pl.multiple_of(s * half, half), half)], gf_v),
        fetch(11, wg, wg_v),
        fetch(12, wu, wu_v),
        fetch(13, wd, wd_v),
    ]

    def remote(src, dst, k, device, recv=None):
        return pltpu.make_async_remote_copy(
            src_ref=src,
            dst_ref=dst,
            send_sem=ssem.at[k],
            recv_sem=rsem.at[k] if recv is None else recv,
            device_id=device,
            device_id_type=MESH,
        )

    def z_send(k, src_of, dst):
        for o in Z_ORDER:
            p = z_peer(o)
            remote(src_of(p), dst.at[z], k, at(x, p)).start()

    def z_bytes(k, buf):
        part = buf.at[pl.ds(0, NZ - 1)]
        return remote(part, part, k, at(x, z_peer(1)))

    def x_send(k, src_of, dst, recv=None):
        for o in X_ORDER:
            p = x_peer(o)
            remote(
                src_of(p), dst.at[x], k, at(p, z), None if recv is None else recv.at[x]
            ).start()

    def x_bytes(k, buf):
        part = buf.at[pl.ds(0, NX - 1)]
        return remote(part, part, k, at(x_peer(1), z))

    def x_wait_one(k, buf, recv, p):
        remote(buf.at[p], buf.at[p], k, at(x_peer(1), z), recv.at[p]).wait_recv()

    def packed(v):
        return block_transpose(widened(v))[:4]

    def unpack_rows(buf, dst):
        for m in range(NZ // 4):
            tile = jnp.concatenate([buf[4 * m + i].astype(F32) for i in range(4)], axis=0)
            dst[:, 128 * m : 128 * m + 128] = block_transpose(tile).astype(BF16)

    got_hid.wait()
    residual = hid_v[...].astype(F32)
    first = packed(residual).astype(BF16)
    h1s[...] = first
    h1r[z] = first
    pl.semaphore_wait(barrier, NZ - 1 + NX - 1 + 1)
    z_send(0, lambda p: h1s, h1r)

    for c in got_first:
        c.wait()
    lanes = 1024
    for c in range(wcat.shape[1] // lanes):
        cols = pl.ds(c * lanes, lanes)
        both = jnp.concatenate([wk_v[:, cols].astype(F32), wv_v[:, cols].astype(F32)], axis=0)
        both = jnp.concatenate([both, jnp.zeros_like(both)], axis=0)
        wcat[rows_q : rows_q + 16, cols] = both.astype(BF16)
    lane1 = iota((1, 128), 1)
    mine = jnp.where(iota(len_v.shape, 1) == z, len_v[...], 0)
    length = jnp.sum(mine, axis=1, keepdims=True)
    cosine, sine = cos_sin(length.astype(F32) * freq_v[...])
    sine = jnp.where(lane1 < HD // 2, -sine, sine)

    z_bytes(0, h1r).wait_recv()
    own_block = xall.at[s, x]
    unpack_rows(h1r, own_block)
    x_send(1, lambda p: own_block, xall.at[s], xr_hid)

    z_send(2, lambda p: ck.at[p], kb)
    z_send(3, lambda p: cv.at[p], vb)

    def forward(p):
        return remote(xall.at[s, p], xall.at[s, p], 4, partner, fwd_r.at[p])

    squares = jnp.zeros((seqs, 128), F32)

    def fold(v):
        v = v * v
        total = v[:, :128]
        for c in range(1, v.shape[1] // 128):
            total = total + v[:, 128 * c : 128 * c + 128]
        return total

    forward(x).start()
    squares = squares + fold(own_block[...].astype(F32))
    for o in X_ARRIVAL:
        p = x_peer(o)
        x_wait_one(1, xall.at[s], xr_hid, p)
        forward(p).start()
        squares = squares + fold(xall[s, p].astype(F32))
    for o in [0] + X_ARRIVAL:
        p = x_peer(o)
        part = xall.at[1 - s, p]
        remote(part, part, 4, partner, fwd_r.at[p]).wait_recv()
        squares = squares + fold(xall[1 - s, p].astype(F32))
    factor = lax.rsqrt(jnp.sum(squares, axis=1, keepdims=True) / (2 * half) + EPS)

    qkv = jnp.zeros((seqs, wcat.shape[0]), F32)
    for h in range(2):
        for p in range(NX):
            cols = pl.ds(h * half + p * block, block)
            normed = (xall[h, p].astype(F32) * factor * ga_v[:, cols]).astype(BF16)
            qkv = qkv + nt_dot(normed, wcat[:, cols])
    qkv = widened(qkv.astype(BF16).astype(F32))
    per = wk_v.shape[0]
    lane = iota((seqs, 128), 1)
    q_row = pltpu.roll(jnp.where(lane < rows_q, qkv, 0.0), rows_q * (z % 4), axis=1)
    k_only = jnp.where((lane >= rows_q) & (lane < rows_q + per), qkv, 0.0)
    v_only = jnp.where((lane >= rows_q + per) & (lane < rows_q + 2 * per), qkv, 0.0)
    kv_row = pltpu.roll(k_only, (128 - rows_q + per * z) % 128, axis=1) + pltpu.roll(
        v_only, (128 - rows_q - per + 64 + per * z) % 128, axis=1
    )
    for b in range(seqs):
        qs[b] = jnp.concatenate([q_row[b : b + 1], kv_row[b : b + 1]], axis=0)
    qr[z] = qs[z]
    z_send(5, lambda p: qs.at[p], qr)
    z_bytes(5, qr).wait_recv()
    heads = [qr[4 * h] + qr[4 * h + 1] + qr[4 * h + 2] + qr[4 * h + 3] for h in range(NZ // 4)]
    kv_sum = heads[0] + heads[1] + heads[2] + heads[3]
    rows = [h[0:1] for h in heads] + [kv_sum[1:2], jnp.zeros((3, 128), F32)]
    message = jnp.concatenate(rows, axis=0).astype(BF16)
    qxs[...] = message
    qxr[x] = message
    x_send(6, lambda p: qxs, qxr)
    x_bytes(6, qxr).wait_recv()

    arrived = [qxr[p].astype(F32) for p in range(NX)]
    kv_rows = [a[4:5] for a in arrived]
    low = lane1 < 64
    new_keys, new_values = [], []
    for k in range(NX // 2):
        a, b = kv_rows[2 * k], kv_rows[2 * k + 1]
        new_keys.append(jnp.where(low, a, pltpu.roll(b, 64, axis=1)))
        new_values.append(jnp.where(low, pltpu.roll(a, 64, axis=1), b))
    nk = len(new_keys)

    def rotated(v):
        return (v * cosine + pltpu.roll(v, HD // 2, axis=1) * sine).astype(BF16)

    query = rotated(jnp.concatenate([a[0:4] for a in arrived], axis=0))
    fill = jnp.zeros((16 - nk, 128), F32)
    kx[...] = rotated(jnp.concatenate(new_keys + [fill], axis=0))
    vx[...] = jnp.concatenate(new_values + [fill], axis=0).astype(BF16)

    for c in got_cache:
        c.wait()
    z_bytes(2, kb).wait_recv()
    n_heads = query.shape[0]
    group = n_heads // nk
    keys = kb[...].reshape(NZ * span, HD)
    cached = nt_dot(query, keys) * (1.0 / math.sqrt(HD))
    own = nt_dot(query, kx[...]) * (1.0 / math.sqrt(HD))
    n_cached = NZ * span
    row_c, lane_c = iota(cached.shape, 0), iota(cached.shape, 1)
    place = x * (n_cached // nk) + lane_c // nk
    live_c = (place < length) & (lane_c % nk == row_c // group)
    row_o, lane_o = iota(own.shape, 0), iota(own.shape, 1)
    live_o = (lane_o == row_o // group) & (x == 0)
    cached = jnp.where(live_c, cached, FLOOR)
    own = jnp.where(live_o, own, FLOOR)
    top = jnp.maximum(
        jnp.max(cached, axis=1, keepdims=True), jnp.max(own, axis=1, keepdims=True)
    )
    w_c = jnp.where(live_c, jnp.exp(cached - top), 0.0)
    w_o = jnp.where(live_o, jnp.exp(own - top), 0.0)
    total = jnp.sum(w_c, axis=1, keepdims=True) + jnp.sum(w_o, axis=1, keepdims=True)
    z_bytes(3, vb).wait_recv()
    values = vb[...].reshape(NZ * span, HD)

    def weighted(w, v):
        high = w.astype(BF16)
        rest = (w - high.astype(F32)).astype(BF16)
        return jnp.dot(high, v, preferred_element_type=F32) + jnp.dot(
            rest, v, preferred_element_type=F32
        )

    mixed = weighted(w_c, values) + weighted(w_o, vx[...])
    lane_h = iota((n_heads, 128), 1)
    stats = jnp.where(lane_h < 64, top, total)
    for p in range(NX):
        ps[p] = jnp.concatenate([mixed[4 * p : 4 * p + 4], stats[4 * p : 4 * p + 4]], axis=0)
    pr[x] = ps[x]
    x_send(7, lambda p: ps.at[p], pr)
    x_bytes(7, pr).wait_recv()
    parts = [pr[p] for p in range(NX)]
    lane4 = iota((4, 128), 1)
    tops, sums = [], []
    for part in parts:
        st = part[4:8]
        turned = pltpu.roll(st, 64, axis=1)
        tops.append(jnp.where(lane4 < 64, st, turned))
        sums.append(jnp.where(lane4 < 64, turned, st))
    highest = tops[0]
    for t in tops[1:]:
        highest = jnp.maximum(highest, t)
    numerator = jnp.zeros((4, 128), F32)
    denominator = jnp.zeros((4, 128), F32)
    for part, t, l in zip(parts, tops, sums):
        scale = jnp.exp(t - highest)
        numerator = numerator + part[0:4] * scale
        denominator = denominator + l * scale
    attended = (numerator / denominator).astype(BF16)
    ats[...] = attended
    atr[z] = attended
    z_send(8, lambda p: ats, atr)
    for c in got_later:
        c.wait()
    z_bytes(8, atr).wait_recv()
    rows4 = [atr[b].astype(F32) for b in range(seqs)]
    for h in range(4):
        axs[:, 128 * h : 128 * h + 128] = jnp.concatenate(
            [r[h : h + 1] for r in rows4], axis=0
        ).astype(BF16)
    x_send(9, lambda p: axs, axr, xr_att)

    def columns(p):
        return pl.ds(pl.multiple_of(p * block, block), block)

    out_part = nt_dot(axs[...], wo_v[:, columns(x)])
    for o in X_ARRIVAL:
        p = x_peer(o)
        x_wait_one(9, axr, xr_att, p)
        out_part = out_part + nt_dot(axr[p], wo_v[:, columns(p)])
    out_part = widened(out_part)
    mos[...] = out_part
    swap = remote(mos, mor, 10, partner)
    swap.start()
    swap.wait_recv()
    both = out_part + mor[...]
    width = hid_v.shape[1]
    both = jnp.where(s == 0, both, pltpu.roll(both, 128 - width, axis=1))
    middle = (residual + both[:, :width]).astype(BF16).astype(F32)

    first = packed(middle).astype(BF16)
    mzs[...] = first
    mzr[z] = first
    z_send(11, lambda p: mzs, mzr)
    z_bytes(11, mzr).wait_recv()
    unpack_rows(mzr, mxs)
    x_send(12, lambda p: mxs, mxr, xr_mid)
    units = wg_v.shape[0]
    gate = jnp.zeros((seqs, units), F32)
    up = jnp.zeros((seqs, units), F32)
    squares = jnp.zeros((seqs, 128), F32)
    for o in [0] + X_ARRIVAL:
        p = x_peer(o)
        if o:
            x_wait_one(12, mxr, xr_mid, p)
            piece = mxr[p].astype(F32)
        else:
            piece = mxs[...].astype(F32)
        squares = squares + fold(piece)
        scaled = (piece * gf_v[:, columns(p)]).astype(BF16)
        gate = gate + nt_dot(scaled, wg_v[:, columns(p)])
        up = up + nt_dot(scaled, wu_v[:, columns(p)])
    ges[0] = widened(gate)
    ges[1] = widened(up)
    ges[2] = squares
    swap2 = remote(ges, ger, 13, partner)
    swap2.start()
    swap2.wait_recv()
    squares = jnp.sum(squares + ger[2], axis=1, keepdims=True)
    factor = lax.rsqrt(squares / (2 * half) + EPS)
    gate = (gate + ger[0][:, :units]) * factor
    up = (up + ger[1][:, :units]) * factor
    hidden = (gate / (1.0 + jnp.exp(-gate)) * up).astype(BF16)
    for o in X_ORDER + [0]:
        p = x_peer(o)
        piece = jnp.dot(hidden, wd_v[:, columns(p)], preferred_element_type=F32).astype(BF16)
        if o:
            dxs[p] = piece
            remote(dxs.at[p], dxr.at[x], 14, at(p, z)).start()
        else:
            dxr[p] = piece
    x_bytes(14, dxr).wait_recv()
    total = dxr[0].astype(F32)
    for p in range(1, NX):
        total = total + dxr[p].astype(F32)
    for m in range(NZ // 4):
        tile = block_transpose(total[:, 128 * m : 128 * m + 128])
        for i in range(4):
            dzs[4 * m + i] = tile[4 * i : 4 * i + 4].astype(BF16)
    dzr[z] = dzs[z]
    z_send(15, lambda p: dzs.at[p], dzr)
    z_bytes(15, dzr).wait_recv()
    total = dzr[0].astype(F32)
    for p in range(1, NZ):
        total = total + dzr[p].astype(F32)
    total = jnp.concatenate([total, jnp.zeros((12, 128), F32)], axis=0)
    down = block_transpose(total)[:, :width]
    out[...] = (middle + down).astype(BF16)

    z_bytes(0, h1r).wait_send()
    x_bytes(1, xall.at[s]).wait_send()
    z_bytes(2, kb).wait_send()
    z_bytes(3, vb).wait_send()
    remote(xall.at[s], xall.at[s], 4, partner).wait_send()
    z_bytes(5, qr).wait_send()
    x_bytes(6, qxr).wait_send()
    x_bytes(7, pr).wait_send()
    z_bytes(8, atr).wait_send()
    x_bytes(9, axr).wait_send()
    swap.wait_send()
    z_bytes(11, mzr).wait_send()
    x_bytes(12, mxr).wait_send()
    swap2.wait_send()
    x_bytes(14, dxr).wait_send()
    z_bytes(15, dzr).wait_send()


def per_device(
    hidden_in, norm_attn, w_query, w_key, w_value, w_out, norm_ffn,
    w_gate, w_up, w_down, cache_keys, cache_values, lengths,
):
    seqs, _, width = hidden_in.shape
    model = w_query.shape[0]
    half = w_gate.shape[1]
    block = half // NX
    units = w_gate.shape[2]
    rows_q, rows_k = w_query.shape[2], w_key.shape[2]
    span, nk = cache_keys.shape[1], cache_keys.shape[2]
    freq = ROPE_BASE ** (-(np.arange(HD // 2, dtype=np.float64) * 2.0) / HD)
    freq = jnp.asarray(np.concatenate([freq, freq])[None].astype(np.float32))
    operands = (
        hidden_in.reshape(seqs, width),
        norm_attn.reshape(1, model),
        w_query.reshape(model, rows_q).T,
        w_key.reshape(model, rows_k).T,
        w_value.reshape(model, rows_k).T,
        w_out.reshape(half, -1).T,
        norm_ffn.reshape(1, model),
        w_gate.reshape(half, units).T,
        w_up.reshape(half, units).T,
        w_down.reshape(units, half),
        cache_keys.reshape(seqs, span * nk, HD),
        cache_values.reshape(seqs, span * nk, HD),
        lengths.reshape(1, seqs),
        freq,
    )
    vm = pltpu.VMEM
    scratch = [
        vm((seqs, width), BF16),
        vm((1, model), F32),
        vm((1, half), F32),
        vm((rows_q + 16, model), BF16),
        vm((rows_k, model), BF16),
        vm((rows_k, model), BF16),
        vm((operands[5].shape[0], half), BF16),
        vm((units, half), BF16),
        vm((units, half), BF16),
        vm((units, half), BF16),
        vm((NZ, span * nk, HD), BF16),
        vm((NZ, span * nk, HD), BF16),
        vm((16, HD), BF16),
        vm((16, HD), BF16),
        vm((1, seqs), jnp.int32),
        vm((1, 128), F32),
        vm((4, 128), BF16),
        vm((NZ, 4, 128), BF16),
        vm((2, NX, seqs, block), BF16),
        vm((seqs, 2, 128), F32),
        vm((NZ, 2, 128), F32),
        vm((8, 128), BF16),
        vm((NX, 8, 128), BF16),
        vm((NX, 8, 128), F32),
        vm((NX, 8, 128), F32),
        vm((4, 128), BF16),
        vm((NZ, 4, 128), BF16),
        vm((seqs, block), BF16),
        vm((NX, seqs, block), BF16),
        vm((seqs, 128), F32),
        vm((seqs, 128), F32),
        vm((4, 128), BF16),
        vm((NZ, 4, 128), BF16),
        vm((seqs, block), BF16),
        vm((NX, seqs, block), BF16),
        vm((3, seqs, 128), F32),
        vm((3, seqs, 128), F32),
        vm((NX, seqs, block), BF16),
        vm((NX, seqs, block), BF16),
        vm((NZ, 4, 128), BF16),
        vm((NZ, 4, 128), BF16),
        pltpu.SemaphoreType.DMA((14,)),
        pltpu.SemaphoreType.DMA((16,)),
        pltpu.SemaphoreType.DMA((16,)),
        pltpu.SemaphoreType.DMA((NX,)),
        pltpu.SemaphoreType.DMA((NX,)),
        pltpu.SemaphoreType.DMA((NX,)),
        pltpu.SemaphoreType.DMA((NX,)),
    ]
    result = pl.pallas_call(
        kernel,
        out_shape=jax.ShapeDtypeStruct((seqs, width), BF16),
        in_specs=[pl.BlockSpec(memory_space=pl.ANY)] * len(operands),
        out_specs=pl.BlockSpec(memory_space=pltpu.VMEM),
        scratch_shapes=scratch,
        compiler_params=pltpu.CompilerParams(
            collective_id=0, has_side_effects=True, vmem_limit_bytes=60 * 1024 * 1024
        ),
    )(*operands)
    return result.reshape(seqs, 1, width)


def solution(mesh):
    return jax.shard_map(
        per_device,
        mesh=mesh,
        in_specs=(
            P("grp", "sub", "tp"),
            P(),
            P(None, "sub", "tp"),
            P(None, "sub", "tp"),
            P(None, "sub", "tp"),
            P("sub", None, None, "tp"),
            P(),
            P("sub", None, "tp"),
            P("sub", None, "tp"),
            P("tp", "sub", None),
            P("grp", "tp", "sub", None),
            P("grp", "tp", "sub", None),
            P("grp"),
        ),
        out_specs=P("grp", "sub", "tp"),
        check_vma=False,
    )
```

time: 598 us -> 125 us (0.21)
  blocking collectives: 341 us -> 0 us
  waiting for transfers between devices: 150 us -> 0 us
  Pallas kernels: 0 us -> 123 us
  local copies, waits for them, and re-layouts: 61.8 us -> 1.28 us
  other arithmetic: 18.1 us -> 0 us
  between operations: 14.3 us -> 0.01 us
    all_gather x6 -> x0, blocking collectives: 331 us -> none  [the longest x4 153 us: gather_in_order(): parts = lax.all_gather(parts, axes[k], axis=0, tiled=True)]
    pallas_call x0 -> x1, Pallas kernels: none -> 123 us  [per_device(): pl.pallas_call(kernel, out_shape=jax.ShapeDtypeStruct((seqs, width), BF16...]
    unnamed x5 -> x0, waiting for transfers between devices: 72.6 us -> none
    squeeze x32 -> x0, local copies, waits for them, and re-layouts: 44.1 us -> none  [the longest x30 41.3 us: combined_by_axis(): array = combine(array, jax.tree.map(lambda part: part[k], pieces))]
    reduce_scatter x1 -> x0, waiting for transfers between devices: 38.7 us -> none  [summed_rows(): array = lax.psum_scatter(array, axis, scatter_dimension=dim, tiled=True)]
    all_gather x2 -> x0, waiting for transfers between devices: 37.7 us -> none  [collected_together(): both, at, found = (lax.all_gather(jnp.concatenate(lines), axis), 0, {})]
    all_to_all x2 -> x0, blocking collectives: 7.48 us -> none  [the longest x1 3.75 us: sent_to_all(): return lax.all_to_all(copies, axis, split_axis=0, concat_axis=0, tiled=True)]
    slice x6 -> x0, local copies, waits for them, and re-layouts: 6.5 us -> none  [the longest x1 3.46 us: combined_by_axis(): array = jax.tree.map(lambda part: part[0], pieces)]
  transfers between devices with their start and end apart: 5 -> 0, of which waited for: 4 -> 0; matrix products, arithmetic and copies ran while one was open for 1% -> 0% of each run, Pallas kernels for 0% -> 0%
where the time goes in v1:
time: 125 us; the launch traced here: 124 us
  Pallas kernels  123 us (98%)
  local copies, waits for them, and re-layouts  1.28 us (1%)
    pallas_call x1, Pallas kernels, per_device(): pl.pallas_call(kernel, out_shape=jax.ShapeDtypeStruct((seqs, width), BF16...  123 us

profile of v1, /device:TPU:80, one launch (start us, length us, event | category | flops | bytes accessed | tf_op | source)
XLA Modules:
  0.0 124.2 jit_solution(9702845155464211315)
XLA Ops:
  0.0 122.9 %shard_map.136 = bf16[16,32]{1,0:T(8,128)(2,1)} custom-call(bf16[16,32]{1,0:T(8,128)(2,1)} %bitcast.38, f32[1,8192]{1,0:T(1,128)} %bitcast.35, bf16[32,8192]{1,0:T(8,128)(2,1)} %bitcast.29, bf16[4,8192]{1,0:T(4,128)(2,1)} %bitcast.33, bf16[4,8192]{1,0:T(4,128)(2,1)} %bitcast.34, bf16[64,4096]{1,0:T(8,128)(2,1)} %bitcast.30, f32[1,8192]{1,0:T(1,128)} %bitcast.36, ...), custom_call_target="tpu_custom_call" | custom-call | tf_op jit(solution)/shard_map/pallas_call | solution.py:514
  122.9 1.3 %copy.16 = bf16[16,1,32]{2,0,1:T(8,128)(2,1)} copy(bf16[16,1,32]{2,0,1:T(8,128)(2,1)} %bitcast.37) | data formatting | bytes 2048

commit v2 on v1

--- a/solution.py
+++ b/solution.py
@@ -67,7 +67,7 @@
     hid_v, ga_v, gf_v, wcat, wk_v, wv_v, wo_v, wg_v, wu_v, wd_v, kb, vb, kx, vx, len_v, freq_v,
     h1s, h1r, xall, qs, qr, qxs, qxr, ps, pr, ats, atr, axs, axr, mos, mor,
     mzs, mzr, mxs, mxr, ges, ger, dxs, dxr, dzs, dzr,
-    local, ssem, rsem, xr_hid, xr_att, xr_mid, fwd_r,
+    local, ssem, rsem, ready, ready_core, ready_row, heard, hz_r, xr_early, xr_hid, xr_att, xr_mid, fwd_r,
 ):
     g, tp, s = lax.axis_index("grp"), lax.axis_index("tp"), lax.axis_index("sub")
     x, z = tp // NZ, tp % NZ
@@ -86,19 +86,37 @@
 
     partner = (g, tp, 1 - s)
 
+    turn = jnp.where((x == 0) & (s == 0), 1, 0)
+    r = (z + NZ - turn) % NZ
+
+    def ranked(k):
+        return at(x, (k + turn) % NZ)
+
+    got_hid = pltpu.make_async_copy(hid, hid_v, local.at[0])
+    got_hid.start()
     barrier = pltpu.get_barrier_semaphore()
-    for o in Z_ORDER:
-        pl.semaphore_signal(barrier, 1, device_id=at(x, z_peer(o)), device_id_type=MESH)
-    for o in X_ORDER:
-        pl.semaphore_signal(barrier, 1, device_id=at(x_peer(o), z), device_id_type=MESH)
-    pl.semaphore_signal(barrier, 1, device_id=partner, device_id_type=MESH)
+    base = z == 1
+
+    @pl.when(s == 1)
+    def _():
+        pl.semaphore_signal(barrier, 1, device_id=partner, device_id_type=MESH)
+
+    for j in range(1, NZ):
+
+        @pl.when(r + j < NZ)
+        def _():
+            pl.semaphore_signal(barrier, 1, device_id=ranked(r + j), device_id_type=MESH)
+
+    @pl.when(base)
+    def _():
+        for o in X_ORDER:
+            pl.semaphore_signal(barrier, 1, device_id=at(x_peer(o), z), device_id_type=MESH)
 
     def fetch(k, src, dst):
         copy = pltpu.make_async_copy(src, dst, local.at[k])
         copy.start()
         return copy
 
-    got_hid = fetch(0, hid, hid_v)
     rows_q = wq.shape[0]
     span = ck.shape[1]
     got_first = [
@@ -157,18 +175,76 @@
     def packed(v):
         return block_transpose(widened(v))[:4]
 
+    def unpacked(chunks):
+        tile = jnp.concatenate([c.astype(F32) for c in chunks], axis=0)
+        return block_transpose(tile).astype(BF16)
+
     def unpack_rows(buf, dst):
         for m in range(NZ // 4):
-            tile = jnp.concatenate([buf[4 * m + i].astype(F32) for i in range(4)], axis=0)
-            dst[:, 128 * m : 128 * m + 128] = block_transpose(tile).astype(BF16)
+            dst[:, 128 * m : 128 * m + 128] = unpacked([buf[4 * m + i] for i in range(4)])
+
+    here = r + (1 - s) + jnp.where(base, NX - 1, 0)
+
+    @pl.when(here > 0)
+    def _():
+        pl.semaphore_wait(barrier, here)
+
+    for j in range(1, NZ):
+
+        @pl.when(j <= r)
+        def _():
+            pl.semaphore_signal(ready.at[r], 1, device_id=ranked(r - j), device_id_type=MESH)
+
+    @pl.when(s == 0)
+    def _():
+        pl.semaphore_signal(ready_core, 1, device_id=partner, device_id_type=MESH)
 
     got_hid.wait()
     residual = hid_v[...].astype(F32)
     first = packed(residual).astype(BF16)
     h1s[...] = first
-    h1r[z] = first
-    pl.semaphore_wait(barrier, NZ - 1 + NX - 1 + 1)
-    z_send(0, lambda p: h1s, h1r)
+    h1r[r] = first
+
+    def chunk(c, src, device):
+        return remote(src, h1r.at[c], 0, device, hz_r.at[c])
+
+    for j in range(NZ - 1, 0, -1):
+
+        @pl.when(j <= r)
+        def _():
+            chunk(r, h1s, ranked(r - j)).start()
+
+    @pl.when(r < NZ - 1)
+    def _():
+        pl.semaphore_wait(ready.at[r + 1], 1)
+        chunk(r, h1s, ranked(r + 1)).start()
+
+    def wait_chunk(c, carry):
+        chunk(c, h1r.at[c], partner).wait_recv()
+        return carry
+
+    lax.fori_loop(0, r, wait_chunk, 0)
+
+    @pl.when(r < NZ - 2)
+    def _():
+        pl.semaphore_wait(ready.at[r + 2], 1)
+
+        def pass_on(c, carry):
+            chunk(c, h1r.at[c], ranked(r + 2)).start()
+            return carry
+
+        lax.fori_loop(0, r + 1, pass_on, 0)
+
+    def send_cache(k):
+        b = (k + turn) % NZ
+        remote(ck.at[b], kb.at[z], 2, ranked(k)).start()
+        remote(cv.at[b], vb.at[z], 3, ranked(k)).start()
+
+    for j in range(1, NZ):
+
+        @pl.when(j <= r)
+        def _():
+            send_cache(r - j)
 
     for c in got_first:
         c.wait()
@@ -184,13 +260,83 @@
     cosine, sine = cos_sin(length.astype(F32) * freq_v[...])
     sine = jnp.where(lane1 < HD // 2, -sine, sine)
 
-    z_bytes(0, h1r).wait_recv()
+    def tell_x_peers(pz):
+        for o in X_ORDER:
+            pl.semaphore_signal(heard.at[pz], 1, device_id=at(x_peer(o), z), device_id_type=MESH)
+
+    def tell_row(pz):
+        pl.semaphore_wait(heard.at[pz], NX - 1)
+        pl.semaphore_signal(ready_row, 1, device_id=at(x, pz), device_id_type=MESH)
+
+    @pl.when(base & (turn == 0))
+    def _():
+        tell_x_peers(0)
+
+    def send_cache_up(ranks):
+        for k in ranks:
+
+            @pl.when(k > r)
+            def _():
+                @pl.when(k > r + 2)
+                def _():
+                    pl.semaphore_wait(ready.at[k], 1)
+
+                send_cache(k)
+
+                @pl.when(base)
+                def _():
+                    tell_x_peers((k + turn) % NZ)
+
+                    @pl.when(k > r + 1)
+                    def _():
+                        tell_row(k + turn - 1)
+
+    send_cache_up(range(1, NZ - 2))
+
     own_block = xall.at[s, x]
-    unpack_rows(h1r, own_block)
-    x_send(1, lambda p: own_block, xall.at[s], xr_hid)
-
-    z_send(2, lambda p: ck.at[p], kb)
-    z_send(3, lambda p: cv.at[p], vb)
+    split = block // 2
+    early = 12 - turn
+    lax.fori_loop(r + 1, early, wait_chunk, 0)
+
+    def unpack_tile(m):
+        to = (m + 3) % 4 * 128
+        chunks = [h1r[(4 * m + i + NZ - turn) % NZ] for i in range(4)]
+        own_block[:, to : to + 128] = unpacked(chunks)
+
+    def half_block(ref, late):
+        return ref.at[:, split * late : split * late + split]
+
+    def x_half(late, recv):
+        for o in X_ORDER:
+            p = x_peer(o)
+            part = half_block(own_block, late)
+            remote(part, part, 1, at(p, z), recv.at[x]).start()
+
+    def x_wait_half(late, recv, p):
+        part = half_block(xall.at[s, p], late)
+        remote(part, part, 1, at(x_peer(1), z), recv.at[p]).wait_recv()
+
+    unpack_tile(1)
+    unpack_tile(2)
+    send_cache_up(range(NZ - 2, NZ))
+
+    @pl.when(base)
+    def _():
+        @pl.when(turn == 0)
+        def _():
+            tell_row(NZ - 1)
+
+        tell_row(0)
+
+    @pl.when(jnp.logical_not(base))
+    def _():
+        pl.semaphore_wait(ready_row, 1)
+
+    x_half(0, xr_early)
+    lax.fori_loop(jnp.maximum(r + 1, early), NZ, wait_chunk, 0)
+    unpack_tile(3)
+    unpack_tile(0)
+    x_half(1, xr_hid)
 
     def forward(p):
         return remote(xall.at[s, p], xall.at[s, p], 4, partner, fwd_r.at[p])
@@ -204,11 +350,16 @@
             total = total + v[:, 128 * c : 128 * c + 128]
         return total
 
+    @pl.when(s == 1)
+    def _():
+        pl.semaphore_wait(ready_core, 1)
+
     forward(x).start()
     squares = squares + fold(own_block[...].astype(F32))
     for o in X_ARRIVAL:
         p = x_peer(o)
-        x_wait_one(1, xall.at[s], xr_hid, p)
+        x_wait_half(0, xr_early, p)
+        x_wait_half(1, xr_hid, p)
         forward(p).start()
         squares = squares + fold(xall[s, p].astype(F32))
     for o in [0] + X_ARRIVAL:
@@ -222,7 +373,9 @@
     for h in range(2):
         for p in range(NX):
             cols = pl.ds(h * half + p * block, block)
-            normed = (xall[h, p].astype(F32) * factor * ga_v[:, cols]).astype(BF16)
+            piece = xall[h, p].astype(F32)
+            piece = jnp.concatenate([piece[:, block - 128 :], piece[:, : block - 128]], axis=1)
+            normed = (piece * factor * ga_v[:, cols]).astype(BF16)
             qkv = qkv + nt_dot(normed, wcat[:, cols])
     qkv = widened(qkv.astype(BF16).astype(F32))
     per = wk_v.shape[0]
@@ -413,7 +566,12 @@
     down = block_transpose(total)[:, :width]
     out[...] = (middle + down).astype(BF16)
 
-    z_bytes(0, h1r).wait_send()
+    def wait_sent(c, carry):
+        chunk(r, h1s, partner).wait_send()
+        return carry
+
+    n_sent = r + jnp.where(r < NZ - 1, 1, 0) + jnp.where(r < NZ - 2, r + 1, 0)
+    lax.fori_loop(0, n_sent, wait_sent, 0)
     x_bytes(1, xall.at[s]).wait_send()
     z_bytes(2, kb).wait_send()
     z_bytes(3, vb).wait_send()
@@ -506,6 +664,12 @@
         pltpu.SemaphoreType.DMA((14,)),
         pltpu.SemaphoreType.DMA((16,)),
         pltpu.SemaphoreType.DMA((16,)),
+        pltpu.SemaphoreType.REGULAR((NZ,)),
+        pltpu.SemaphoreType.REGULAR,
+        pltpu.SemaphoreType.REGULAR,
+        pltpu.SemaphoreType.REGULAR((NZ,)),
+        pltpu.SemaphoreType.DMA((NZ,)),
+        pltpu.SemaphoreType.DMA((NX,)),
         pltpu.SemaphoreType.DMA((NX,)),
         pltpu.SemaphoreType.DMA((NX,)),
         pltpu.SemaphoreType.DMA((NX,)),

time: 125 us -> 117 us (0.936)
  Pallas kernels: 123 us -> 116 us
    pallas_call x1, Pallas kernels: 123 us -> 116 us  [per_device(): pl.pallas_call(kernel, out_shape=jax.ShapeDtypeStruct((seqs, width), BF16...]
where the time goes in v2:
time: 117 us
  Pallas kernels  116 us (99%)
  local copies, waits for them, and re-layouts  1.28 us (1%)
    pallas_call x1, Pallas kernels, per_device(): pl.pallas_call(kernel, out_shape=jax.ShapeDtypeStruct((seqs, width), BF16...  116 us

profile of v2, /device:TPU:80, one launch (start us, length us, event | category | flops | bytes accessed | tf_op | source)
XLA Modules:
  0.0 117.3 jit_solution(7271493707282357760)
XLA Ops:
  0.0 116.0 %shard_map.136 = bf16[16,32]{1,0:T(8,128)(2,1)} custom-call(bf16[16,32]{1,0:T(8,128)(2,1)} %bitcast.38, f32[1,8192]{1,0:T(1,128)} %bitcast.35, bf16[32,8192]{1,0:T(8,128)(2,1)} %bitcast.29, bf16[4,8192]{1,0:T(4,128)(2,1)} %bitcast.33, bf16[4,8192]{1,0:T(4,128)(2,1)} %bitcast.34, bf16[64,4096]{1,0:T(8,128)(2,1)} %bitcast.30, f32[1,8192]{1,0:T(1,128)} %bitcast.36, ...), custom_call_target="tpu_custom_call" | custom-call | tf_op jit(solution)/shard_map/pallas_call | solution.py:678
  116.0 1.3 %copy.16 = bf16[16,1,32]{2,0,1:T(8,128)(2,1)} copy(bf16[16,1,32]{2,0,1:T(8,128)(2,1)} %bitcast.37) | data formatting | bytes 2048
